TPU v7x, 32 devices: a whole 2x2x4 slice. The times are simulated.
32 devices in a mesh: rep: 1, ep: 32 (over z, y, x, core).
Axes of the slice: x: 2, y: 2, z: 4, core: 2. Of those that a mesh axis runs over, the one named last changes fastest.
Arguments:
- tokens: bfloat16 [512, 3584], P(('rep', 'ep')), may hold values from -6 to 6
- routes: int32 [512, 8], P(('rep', 'ep')), may hold values from 0 to 15, all different within a row; in each aligned block of 16 rows (0 to 15, 16 to 31, ...) at most 16 rows name the same one
- gate_weights: float32 [512, 8], P(('rep', 'ep')), may hold values from 0.05 to 0.5
- w_gate: bfloat16 [32, 3584, 512], P('ep'), may hold values from -0.09375 to 0.09375
- w_up: bfloat16 [32, 3584, 512], P('ep'), may hold values from -0.09375 to 0.09375
- w_down: bfloat16 [32, 512, 3584], P('ep'), may hold values from -0.1875 to 0.1875
Outputs:
- mixed: bfloat16 [512, 3584], P(('rep', 'ep'))
Inputs may be any that keep to these rules, and one draw needn't show every extreme that they name: `routes`: each token names 8 different experts. Among the tokens of one device at most 16 name any one expert, and in every draw some expert is named by exactly 16 tokens of some device.
All inputs are finite; a program needn't handle non-finite values.
Results may differ from a plain program's by a relative error of at most 0.008.
Values may be sent and summed in bfloat16 or wider, within the bound.
A program may use at most 128 MiB of HBM per device.

v0:
```python
import jax
import jax.numpy as jnp
from jax import lax
from jax.sharding import PartitionSpec as P


def swapped(value, axis, bit):
    mask = 2**bit
    pairs = [(source, source ^ mask) for source in range(lax.axis_size(axis))]
    return lax.ppermute(value, axis, pairs)


def slot_positions(chosen, expert_count):
    chosen_hits = jnp.sum(
        (chosen[:, :, None] == jnp.arange(expert_count, dtype=jnp.int32)[None, None, :]).astype(
            jnp.int32
        ),
        axis=1,
        dtype=jnp.int32,
    )
    before = jnp.cumsum(chosen_hits, axis=0, dtype=jnp.int32) - chosen_hits
    return jnp.take_along_axis(before, chosen, axis=1)


def expert_half(expert_rows, w_gate, w_up, w_down):
    gate_value = jnp.dot(expert_rows, w_gate[0], preferred_element_type=jnp.float32)
    up_value = jnp.dot(expert_rows, w_up[0], preferred_element_type=jnp.float32)
    hidden = (jax.nn.silu(gate_value) * up_value).astype(jnp.bfloat16)
    return jnp.dot(hidden, w_down[0], preferred_element_type=jnp.float32).astype(jnp.bfloat16)


def body(tokens, routes, gate_weights, w_gate, w_up, w_down):
    row_count = tokens.shape[0]
    top_count = routes.shape[1]
    width = tokens.shape[1]
    devices = lax.axis_size("ep")
    expert_count = devices // 2
    capacity = min(row_count, 2 * row_count * top_count // expert_count)
    half_cap = capacity // 2
    parity = lax.axis_index("ep") % 2
    slot_index = slot_positions(routes, expert_count)
    flat_index = (routes * capacity + slot_index).reshape(-1)
    buffer = (
        jnp.zeros((expert_count * capacity, width), jnp.bfloat16)
        .at[flat_index]
        .set(jnp.repeat(tokens, top_count, axis=0))
    )
    buffer = buffer.reshape(expert_count, capacity, width)
    outgoing = buffer.reshape(devices, half_cap, width)
    own_half = lax.all_to_all(outgoing, "ep", split_axis=0, concat_axis=0, tiled=True)
    partner_half = swapped(own_half, "ep", 0)
    lower_half = jnp.where(parity == 0, own_half, partner_half)
    upper_half = jnp.where(parity == 0, partner_half, own_half)
    arrived = jnp.concatenate([lower_half, upper_half], axis=1)
    expert_rows = arrived.reshape(devices * capacity, width)
    partial_value = expert_half(expert_rows, w_gate, w_up, w_down).reshape(devices, capacity, width)
    returned = lax.all_to_all(partial_value, "ep", split_axis=0, concat_axis=0, tiled=True)
    paired = returned.reshape(expert_count, 2, capacity, width)
    expert_out = (paired[:, 0].astype(jnp.float32) + paired[:, 1].astype(jnp.float32)).astype(
        jnp.bfloat16
    )
    table = expert_out.reshape(expert_count * capacity, width)
    picked = table[flat_index].reshape(row_count, top_count, width).astype(jnp.float32)
    mixed = jnp.einsum("tk,tkd->td", gate_weights, picked)
    return mixed.astype(jnp.bfloat16)


def solution(mesh):
    placed = (
        P(("rep", "ep"), None),
        P(("rep", "ep"), None),
        P(("rep", "ep"), None),
        P("ep", None, None),
        P("ep", None, None),
        P("ep", None, None),
    )
    return jax.shard_map(
        body, mesh=mesh, in_specs=placed, out_specs=P(("rep", "ep"), None), check_vma=False
    )
```

profile of v0, /device:TPU:0, one launch (start us, length us, event | category | flops | bytes accessed | tf_op | source)
XLA Modules:
  0.0 168.6 jit_solution(2942011848193091434)
XLA Ops:
  0.0 0.0 copy-start
  0.0 0.8 copy.19
  0.8 0.7 bitcast_or_fusion
  1.5 0.1 convert_reduce_fusion
  1.6 0.1 copy.20
  1.7 0.1 reshape.78
  1.8 0.0 copy-start.2
  1.8 1.3 gather_fusion.1
  3.1 0.1 reshape.81
  3.2 0.1 copy.21
  3.2 0.0 copy-done.2
  3.2 0.1 copy.22
  3.3 0.1 reshape.64
  3.4 0.0 copy-done
  3.4 2.5 %scatter_custom_fusion = bf16[256,3584]{1,0:T(8,128)(2,1)S(1)} fusion(s32[128]{0:T(128)S(1)} %fusion.16, bf16[]{:T(256)} %constant.39.clone.1, bf16[16,3584]{1,0:T(8,128)(2,1)S(1)} %copy-done), kind=kCustom, calls=%fused_computation.18 | custom fusion | bytes 1949698 | tf_op jit(solution)/shard_map/scatter | solution.py:46
  5.9 50.3 %all_to_all.10 = bf16[32,8,3584]{2,1,0:T(8,128)(2,1)} all-to-all(bf16[32,8,3584]{2,1,0:T(8,128)(2,1)S(1)} %bitcast.46), channel_id=1, replica_groups=mesh['rep'=1,'ep'=32] {'ep'}, dimensions={0} | all-to-all | bytes 3670016 | tf_op jit(solution)/shard_map/all_to_all | solution.py:50
  56.2 0.0 collective-permute-start
  56.2 4.0 %collective-permute-done = bf16[32,8,3584]{2,1,0:T(8,128)(2,1)S(1)} collective-permute-done((bf16[32,8,3584]{2,1,0:T(8,128)(2,1)}, bf16[32,8,3584]{2,1,0:T(8,128)(2,1)S(1)}, u32[]{:S(2)}, u32[]{:S(2)}) %collective-permute-start) | collective-permute-done | bytes 1835040 | tf_op jit(solution)/shard_map/ppermute | solution.py:10
  60.2 1.7 %broadcast_select_fusion.1 = (bf16[32,8,3584]{2,1,0:T(8,128)(2,1)S(1)}, bf16[32,8,3584]{2,1,0:T(8,128)(2,1)S(1)}) fusion(bf16[32,8,3584]{2,1,0:T(8,128)(2,1)} %all_to_all.10, bf16[32,8,3584]{2,1,0:T(8,128)(2,1)S(1)} %collective-permute-done, pred[]{:T(512)S(6)} %eq.10), kind=kLoop, calls=%fused_computation.14 | loop fusion | flops 1835008 | bytes 7340033 | tf_op jit(solution)/shard_map/jit(_where)/select_n | solution.py:52
  62.0 0.0 copy-start.4
  62.0 0.5 pad_maximum_fusion
  62.5 1.9 %copy-done.1 = bf16[32,16,3584]{2,1,0:T(8,128)(2,1)} copy-done((bf16[32,16,3584]{2,1,0:T(8,128)(2,1)}, bf16[32,16,3584]{2,1,0:T(8,128)(2,1)S(1)}, u32[]{:S(2)}) %copy-start.1) | copy-done | bytes 3670040
  64.3 1.0 copy-done.4
  65.3 2.0 %fusion.1 = f32[512,512]{1,0:T(8,128)S(1)} fusion(bf16[512,3584]{1,0:T(8,128)(2,1)S(1)} %bitcast.48, bf16[1,3584,512]{2,1,0:T(8,128)(2,1)S(1)} %copy-done.4), kind=kOutput, calls=%fused_computation.6 | convolution fusion | flops 1879048192 | bytes 8388608 | tf_op jit(solution)/shard_map/dot_general | solution.py:27
  67.4 10.1 %convolution_convert_fusion = bf16[512,3584]{1,0:T(8,128)(2,1)} fusion(bf16[1,512,3584]{2,1,0:T(8,128)(2,1)} %param.11, f32[512,512]{1,0:T(8,128)S(1)} %fusion.1, bf16[512,3584]{1,0:T(8,128)(2,1)} %bitcast.49, bf16[1,3584,512]{2,1,0:T(8,128)(2,1)} %param.9), kind=kOutput, calls=%fused_computation.3 | convolution fusion | flops 3761504256 | bytes 15728640 | tf_op jit(solution)/shard_map/dot_general | solution.py:29
  77.5 3.7 %all-to-all-start.1 = ((bf16[32,16,3584]{2,1,0:T(8,128)(2,1)}), bf16[32,16,3584]{2,1,0:T(8,128)(2,1)}, u32[]{:S(2)}, u32[]{:S(2)}) async-start(bf16[32,16,3584]{2,1,0:T(8,128)(2,1)} %bitcast.47), calls=%async_computation.1 | async-start | bytes 7340032 | tf_op jit(solution)/shard_map/all_to_all | solution.py:57
  81.3 0.1 copy.25
  81.3 82.4 %all-to-all-done.1 = bf16[32,16,3584]{2,1,0:T(8,128)(2,1)} async-done(((bf16[32,16,3584]{2,1,0:T(8,128)(2,1)}), bf16[32,16,3584]{2,1,0:T(8,128)(2,1)}, u32[]{:S(2)}, u32[]{:S(2)}) %all-to-all-start.1) | async-done | bytes 3670048 | tf_op jit(solution)/shard_map/all_to_all | solution.py:57
  163.8 2.6 %add_convert_fusion = bf16[16,1,16,3584]{3,2,0,1:T(8,128)(2,1)S(1)} fusion(bf16[16,2,16,3584]{3,2,1,0:T(8,128)(2,1)} %bitcast.9), kind=kLoop, calls=%fused_computation.10 | loop fusion | flops 3670016 | bytes 5505024 | tf_op jit(solution)/shard_map/convert_element_type | solution.py:59
  166.4 1.1 gather_fusion
  167.5 0.4 fusion.5
  167.9 0.7 copy.30
  (8 shorter events, 0.1 us)
Async XLA Ops:
  0.0 3.4 %copy-start = (bf16[16,3584]{1,0:T(8,128)(2,1)S(1)}, bf16[16,3584]{1,0:T(8,128)(2,1)}, u32[]{:S(2)}) copy-start(bf16[16,3584]{1,0:T(8,128)(2,1)} %param.6) | copy-start | bytes 344068
  1.8 1.4 copy-start.2
  56.2 4.0 %collective-permute-start = (bf16[32,8,3584]{2,1,0:T(8,128)(2,1)}, bf16[32,8,3584]{2,1,0:T(8,128)(2,1)S(1)}, u32[]{:S(2)}, u32[]{:S(2)}) collective-permute-start(bf16[32,8,3584]{2,1,0:T(8,128)(2,1)} %all_to_all.10), channel_id=1, source_target_pairs={{0,1},{1,0},{2,3},{3,2},{4,5},{5,4},{6,7},{7,6},{8,9},{9,8},{10,11... | collective-permute-start | bytes 5505032 | tf_op jit(solution)/shard_map/ppermute | solution.py:10
  62.0 3.4 %copy-start.4 = (bf16[1,3584,512]{2,1,0:T(8,128)(2,1)S(1)}, bf16[1,3584,512]{2,1,0:T(8,128)(2,1)}, u32[]{:S(2)}) copy-start(bf16[1,3584,512]{2,1,0:T(8,128)(2,1)} %param.10) | copy-start | bytes 11010052
  62.5 1.9 %copy-start.1 = (bf16[32,16,3584]{2,1,0:T(8,128)(2,1)}, bf16[32,16,3584]{2,1,0:T(8,128)(2,1)S(1)}, u32[]{:S(2)}) copy-start(bf16[32,16,3584]{2,1,0:T(8,128)(2,1)S(1)} %pad_maximum_fusion) | copy-start | bytes 11010052
  77.5 3.7 %copy-start.3 = (f32[16,8]{0,1:T(8,128)S(1)}, f32[16,8]{0,1:T(8,128)}, u32[]{:S(2)}) copy-start(f32[16,8]{0,1:T(8,128)} %param.8) | copy-start | bytes 1540
  77.5 86.3 %all-to-all-start.1 = ((bf16[32,16,3584]{2,1,0:T(8,128)(2,1)}), bf16[32,16,3584]{2,1,0:T(8,128)(2,1)}, u32[]{:S(2)}, u32[]{:S(2)}) async-start(bf16[32,16,3584]{2,1,0:T(8,128)(2,1)} %bitcast.47), calls=%async_computation.1 | async-start | bytes 7340032 | tf_op jit(solution)/shard_map/all_to_all | solution.py:57
where the time goes:
time: 169 us
  waiting for transfers between devices  86.4 us (51%)
  blocking collectives  50.3 us (30%)
  matrix products  12.6 us (7%)
  local copies, waits for them, and re-layouts  9.75 us (6%)
  other arithmetic  5.7 us (3%)
  starting transfers between devices  3.74 us (2%)
    all_to_all x1, waiting for transfers between devices, body(): lax.all_to_all(partial_value, 'ep', split_axis=0, concat_axis=0, tiled=True)  82.4 us
    all_to_all x1, blocking collectives, body(): lax.all_to_all(outgoing, 'ep', split_axis=0, concat_axis=0, tiled=True)  50.3 us
    dot_general x1, matrix products, expert_half(): jnp.dot(hidden, w_down[0], preferred_element_type=jnp.float32)  10.1 us
    ppermute x1, waiting for transfers between devices, swapped(): return lax.ppermute(value, axis, pairs)  3.99 us
    unnamed x12, local copies, waits for them, and re-layouts  3.75 us
    all_to_all x1, starting transfers between devices, body(): lax.all_to_all(partial_value, 'ep', split_axis=0, concat_axis=0, tiled=True)  3.73 us
  transfers between devices with their start and end apart: 2, of which 2 were waited for; matrix products, arithmetic and copies ran while one was open for 0% of the time, Pallas kernels for 0%

commit v1 on v0

v1 whole, which is shorter than its diff:
```python
import jax
import jax.numpy as jnp
from jax import lax
from jax.sharding import PartitionSpec as P


def dense_gates(routes, gate_weights, expert_count):
    hit = routes[:, :, None] == jnp.arange(expert_count, dtype=jnp.int32)[None, None, :]
    return jnp.sum(jnp.where(hit, gate_weights[:, :, None], 0.0), axis=1)


def body(tokens, routes, gate_weights, w_gate, w_up, w_down):
    devices = lax.axis_size("ep")
    expert_count = devices // 2
    expert = lax.axis_index("ep") // 2
    gates = dense_gates(routes, gate_weights, expert_count)
    all_gates = lax.all_gather(gates, "ep", axis=0, tiled=True)
    mine = lax.dynamic_slice_in_dim(all_gates, expert, 1, axis=1)
    rows = lax.all_gather(tokens, "ep", axis=0, tiled=True)
    gate_value = jnp.dot(rows, w_gate[0], preferred_element_type=jnp.float32)
    up_value = jnp.dot(rows, w_up[0], preferred_element_type=jnp.float32)
    hidden = (jax.nn.silu(gate_value) * up_value * mine).astype(jnp.bfloat16)
    partial_value = jnp.dot(hidden, w_down[0], preferred_element_type=jnp.float32)
    return lax.psum_scatter(
        partial_value.astype(jnp.bfloat16), "ep", scatter_dimension=0, tiled=True
    )


def solution(mesh):
    placed = (
        P(("rep", "ep"), None),
        P(("rep", "ep"), None),
        P(("rep", "ep"), None),
        P("ep", None, None),
        P("ep", None, None),
        P("ep", None, None),
    )
    return jax.shard_map(
        body, mesh=mesh, in_specs=placed, out_specs=P(("rep", "ep"), None), check_vma=False
    )
```

time: 169 us -> 236 us (1.40)
  waiting for transfers between devices: 86.4 us -> 161 us
  between operations: 0.14 us -> 13.4 us
  local copies, waits for them, and re-layouts: 9.75 us -> 1.75 us
  blocking collectives: 50.3 us -> 44.3 us
  other arithmetic: 5.7 us -> 0.11 us
  starting transfers between devices: 3.74 us -> 0.04 us
  matrix products: 12.6 us -> 15.3 us
    reduce_scatter x0 -> x1, waiting for transfers between devices: none -> 140 us  [body(): lax.psum_scatter(partial_value.astype(jnp.bfloat16), 'ep', scatter_dimens...]
    all_to_all x1 -> x0, waiting for transfers between devices: 82.4 us -> none  [body(): lax.all_to_all(partial_value, 'ep', split_axis=0, concat_axis=0, tiled=True)]
    all_to_all x1 -> x0, blocking collectives: 50.3 us -> none  [body(): lax.all_to_all(outgoing, 'ep', split_axis=0, concat_axis=0, tiled=True)]
    all_gather x0 -> x1, blocking collectives: none -> 44.3 us  [body(): all_gates = lax.all_gather(gates, 'ep', axis=0, tiled=True)]
    all_gather x0 -> x1, waiting for transfers between devices: none -> 20 us  [body(): rows = lax.all_gather(tokens, 'ep', axis=0, tiled=True)]
    ppermute x1 -> x0, waiting for transfers between devices: 3.99 us -> none  [swapped(): return lax.ppermute(value, axis, pairs)]
    all_to_all x1 -> x0, starting transfers between devices: 3.73 us -> none  [body(): lax.all_to_all(partial_value, 'ep', split_axis=0, concat_axis=0, tiled=True)]
    dot_general x3 -> x2, matrix products: 12.6 us -> 15.3 us  [the longest x1 10.1 us: body(): jnp.dot(hidden, w_down[0], preferred_element_type=jnp.float32)]
  transfers between devices with their start and end apart: 2 -> 2, of which waited for: 2 -> 2; matrix products, arithmetic and copies ran while one was open for 0% -> 1% of each run, Pallas kernels for 0% -> 0%
where the time goes in v1:
time: 236 us
  waiting for transfers between devices  161 us (68%)
  blocking collectives  44.3 us (19%)
  matrix products  15.3 us (6%)
  between operations  13.4 us (6%)
    reduce_scatter x1, waiting for transfers between devices, body(): lax.psum_scatter(partial_value.astype(jnp.bfloat16), 'ep', scatter_dimens...  140 us
    all_gather x1, blocking collectives, body(): all_gates = lax.all_gather(gates, 'ep', axis=0, tiled=True)  44.3 us
    all_gather x1, waiting for transfers between devices, body(): rows = lax.all_gather(tokens, 'ep', axis=0, tiled=True)  20 us
    dot_general x1, matrix products, body(): jnp.dot(hidden, w_down[0], preferred_element_type=jnp.float32)  10.1 us
    dot_general x1, matrix products, body(): gate_value = jnp.dot(rows, w_gate[0], preferred_element_type=jnp.float32)  5.21 us
  transfers between devices with their start and end apart: 2, of which 2 were waited for; matrix products, arithmetic and copies ran while one was open for 1% of the time, Pallas kernels for 0%

profile of v1, /device:TPU:0, one launch (start us, length us, event | category | flops | bytes accessed | tf_op | source)
XLA Modules:
  0.0 235.8 jit_solution(9935456027854228709)
XLA Ops:
  6.5 0.0 all-gather.2.cloned.1.call-start
  6.5 0.7 all-gather.2.cloned.1.call-update
  7.3 0.0 reduce-scatter.2.cloned.1.call-start
  7.3 0.8 copy.13
  8.1 0.8 copy.14
  8.8 0.1 select_reduce_fusion
  8.9 44.3 %all_gather.7 = f32[512,16]{1,0:T(8,128)S(1)} all-gather(f32[16,16]{1,0:T(8,128)S(1)} %select_reduce_fusion), channel_id=1, replica_groups=mesh['rep'=1,'ep'=32] {'ep'}, dimensions={0}, use_global_device_ids=true | all-gather | bytes 33792 | tf_op jit(solution)/shard_map/all_gather | solution.py:17
  53.2 0.2 dynamic-slice_reduce_fusion
  53.4 20.0 %all-gather.2.cloned.1.call-done = bf16[512,3584]{1,0:T(8,128)(2,1)} async-done(((bf16[16,3584]{1,0:T(8,128)(2,1)}), bf16[512,3584]{1,0:T(8,128)(2,1)}) %all-gather.2.cloned.1.call-update) | async-done | bytes 3670032 | tf_op jit(solution)/shard_map/all_gather | solution.py:19
  73.4 5.2 %fusion.3 = f32[512,512]{1,0:T(8,128)S(1)} fusion(bf16[512,3584]{1,0:T(8,128)(2,1)} %all-gather.2.cloned.1.call-done, bf16[1,3584,512]{2,1,0:T(8,128)(2,1)} %param.9), kind=kOutput, calls=%fused_computation.4 | convolution fusion | flops 1879048192 | bytes 8388608 | tf_op jit(solution)/shard_map/dot_general | solution.py:20
  78.6 10.1 %convolution_convert_fusion = bf16[512,3584]{1,0:T(8,128)(2,1)} fusion(bf16[1,512,3584]{2,1,0:T(8,128)(2,1)} %param.11, bf16[512,3584]{1,0:T(8,128)(2,1)} %all-gather.2.cloned.1.call-done, bf16[1,3584,512]{2,1,0:T(8,128)(2,1)} %param.10, f32[512,512]{1,0:T(8,128)S(1)} %fusion.3, f32[512]{0:T(512)S(1)} %dynamic-slice_reduce_fusion), kind=kOutput, calls=%fused_computation | convolution fusion | flops 3761766400 | bytes 15730688 | tf_op jit(solution)/shard_map/dot_general | solution.py:23
  88.7 0.0 reduce-scatter.2.cloned.1.call-update
  88.7 140.2 %reduce-scatter.2.cloned.1.call-done = bf16[16,3584]{1,0:T(8,128)(2,1)} async-done(((bf16[512,3584]{1,0:T(8,128)(2,1)}), bf16[16,3584]{1,0:T(8,128)(2,1)}) %reduce-scatter.2.cloned.1.call-update) | async-done | bytes 114704 | tf_op jit(solution)/shard_map/reduce_scatter | solution.py:24
Async XLA Ops:
  6.5 66.9 %all-gather.2.cloned.1.call-start = ((), (), s32[]{:S(2)}) async-start(), calls=%async_computation.1 | async-start | bytes 3784704 | tf_op jit(solution)/shard_map/all_gather | solution.py:19
  7.3 221.7 %reduce-scatter.2.cloned.1.call-start = ((), (), s32[]{:S(2)}) async-start(), calls=%async_computation.2 | async-start | bytes 3784704 | tf_op jit(solution)/shard_map/reduce_scatter | solution.py:24
Sparse Core Ops, SparseCore 0:
  10.2 63.1 all-gather.1
  88.9 140.0 reduce-scatter.1

commit v2 on v1

v2 whole, which is shorter than its diff:
```python
import functools

import jax
import jax.numpy as jnp
from jax import lax
from jax.experimental import pallas as pl
from jax.experimental.pallas import tpu as pltpu
from jax.sharding import PartitionSpec as P

F32 = jnp.float32
BF16 = jnp.bfloat16
PLANE = 4
KINDS = 15
(Z_ROWS, X_ROWS, Y_ROWS, D_LOW, D_HIGH, TWIN, _, _, _, PAIR, S_LOW, S_HIGH, S_X, S_Y, S_Z) = range(KINDS)


def pack_width(expert_count):
    return -(-3 * expert_count // 128) * 128


def packed_gates(routes, weights, expert_count, lanes):
    rows, top = routes.shape
    lane = lax.broadcasted_iota(jnp.int32, (rows, lanes), 1)
    expert = jnp.where(lane >= 2 * expert_count, lane - 2 * expert_count, jnp.where(lane >= expert_count, lane - expert_count, lane))
    dense = jnp.zeros((rows, lanes), F32)
    for k in range(top):
        dense = dense + jnp.where(routes[:, k : k + 1] == expert, weights[:, k : k + 1], 0.0)
    high = dense.astype(BF16).astype(F32)
    middle = (dense - high).astype(BF16).astype(F32)
    low = dense - high - middle
    piece = jnp.where(lane < expert_count, high, jnp.where(lane < 2 * expert_count, middle, low))
    return jnp.where(lane < 3 * expert_count, piece, 0.0).astype(BF16)


def kernel(
    devices, tokens, routes, weights, w_gate, w_up, w_down, out,
    tok, wg, wu, wd, hid, p_own, p_out, p_in, diag, low_in, high_in,
    to_x, to_y, from_x, from_y, to_z, from_z, kept, load_sem, send_sem, recv_sem,
):
    rows, width = out.shape
    planes = devices // (2 * PLANE)
    expert_count = devices // 2
    wide = tok.shape[1]
    half_w = wide // 256 * 128
    half_d = width // 256 * 128
    chunk = 2 * PLANE * rows
    near = PLANE * rows
    me = lax.axis_index("ep")
    twin = me + 1 - 2 * (me % 2)
    x_mate = me + 2 - 4 * ((me // 2) % 2)
    y_mate = me + 4 - 8 * ((me // 4) % 2)
    z, inside = me // (2 * PLANE), me % (2 * PLANE)

    def z_mate(step):
        return ((z + step) % planes) * (2 * PLANE) + inside

    loads = [
        pltpu.make_async_copy(tokens, tok.at[pl.ds(0, rows), pl.ds(0, width)], load_sem.at[0]),
        pltpu.make_async_copy(w_gate.at[0], wg, load_sem.at[1]),
        pltpu.make_async_copy(w_up.at[0], wu, load_sem.at[2]),
        pltpu.make_async_copy(w_down.at[0], wd, load_sem.at[3]),
    ]
    for load in loads:
        load.start()
    barrier = pltpu.get_barrier_semaphore()
    mates = [twin, x_mate, y_mate] + [z_mate(s) for s in range(1, planes)]
    for mate in mates:
        pl.semaphore_signal(barrier, inc=1, device_id={"ep": mate}, device_id_type=pl.DeviceIdType.MESH)
    tok[pl.ds(0, rows), pl.ds(width, wide - width)] = packed_gates(routes[...], weights[...], expert_count, wide - width)
    loads[0].wait()
    pl.semaphore_wait(barrier, len(mates))

    copies = {}

    def send(kind, s, source, target, device):
        copy = pltpu.make_async_remote_copy(
            src_ref=source, dst_ref=target,
            send_sem=send_sem.at[kind, s], recv_sem=recv_sem.at[kind, s],
            device_id={"ep": device}, device_id_type=pl.DeviceIdType.MESH,
        )
        copy.start()
        copies[kind, s] = copy

    def arrived(kind, s):
        copies[kind, s].wait_recv()

    def block(s, k, r, first=0, size=None):
        return tok.at[pl.ds(((s * 2 + k) * PLANE + r) * rows, rows), pl.ds(first, wide if size is None else size)]

    def to_twin(s, r):
        send(TWIN + r, s, block(s, 0, r), block(s, 1, r), twin)

    def gather_own(s):
        if s:
            arrived(Z_ROWS, s)
        send(X_ROWS, s, block(s, 0, 0), block(s, 0, 1), x_mate)
        send(Y_ROWS, s, block(s, 0, 0), block(s, 0, 2), y_mate)
        to_twin(s, 0)

    def gather_side(s):
        arrived(X_ROWS, s)
        send(D_LOW, s, block(s, 0, 1, 0, half_w), block(s, 0, 3, 0, half_w), y_mate)
        arrived(Y_ROWS, s)
        send(D_HIGH, s, block(s, 0, 2, half_w, wide - half_w), block(s, 0, 3, half_w, wide - half_w), x_mate)
        to_twin(s, 1)
        to_twin(s, 2)

    def gather_diag(s):
        arrived(D_LOW, s)
        arrived(D_HIGH, s)
        to_twin(s, 3)

    def compute(s):
        for r in range(PLANE):
            arrived(TWIN + r, s)
        here = pl.ds(s * chunk, chunk)
        if s == 0:
            loads[1].wait()
            loads[2].wait()
        lanes = wide - width
        lane = lax.broadcasted_iota(jnp.int32, (chunk, lanes), 1)
        expert = me // 2
        mine = (lane == expert) | (lane == expert + expert_count) | (lane == expert + 2 * expert_count)
        scale = jnp.sum(jnp.where(mine, tok[here, pl.ds(width, lanes)].astype(F32), 0.0), axis=1, keepdims=True)
        hidden_count = wg.shape[1]
        piece = min(256, hidden_count)

        def hidden_piece(j, carry):
            cols = pl.ds(pl.multiple_of(j * piece, piece), piece)
            gate = jnp.dot(tok[here, pl.ds(0, width)], wg[:, cols], preferred_element_type=F32)
            up = jnp.dot(tok[here, pl.ds(0, width)], wu[:, cols], preferred_element_type=F32)
            hid[:, cols] = (jax.nn.silu(gate) * up * scale).astype(BF16)
            return carry

        lax.fori_loop(0, hidden_count // piece, hidden_piece, 0)
        if s == 0:
            loads[3].wait()
        span = 512 if width % 512 == 0 else 128

        def down_piece(j, carry):
            cols = pl.ds(pl.multiple_of(j * span, span), span)
            part = jnp.dot(hid[...], wd[:, cols], preferred_element_type=F32)
            p_own[pl.ds(s * near, near), cols] = part[:near]
            p_out[pl.ds(s * near, near), cols] = part[near:].astype(BF16)
            return carry

        lax.fori_loop(0, width // span, down_piece, 0)
        send(PAIR, s, p_out.at[pl.ds(s * near, near), :], p_in.at[pl.ds(s * near, near), :], twin)

    def slab(s):
        return pl.ds(s * rows, rows)

    def both(s, r):
        at = pl.ds(s * near + r * rows, rows)
        return p_own[at, :] + p_in[at, :].astype(F32)

    def scatter_diag(s):
        arrived(PAIR, s)
        diag[slab(s), :] = both(s, 3).astype(BF16)
        send(S_LOW, s, diag.at[slab(s), pl.ds(0, half_d)], low_in.at[slab(s), :], y_mate)
        send(S_HIGH, s, diag.at[slab(s), pl.ds(half_d, width - half_d)], high_in.at[slab(s), :], x_mate)

    def scatter_side(s):
        for_x, for_y = both(s, 1), both(s, 2)
        arrived(S_LOW, s)
        to_x[slab(s), pl.ds(0, half_d)] = (for_x[:, :half_d] + low_in[slab(s), :].astype(F32)).astype(BF16)
        to_x[slab(s), pl.ds(half_d, width - half_d)] = for_x[:, half_d:].astype(BF16)
        send(S_X, s, to_x.at[slab(s), :], from_x.at[slab(s), :], x_mate)
        arrived(S_HIGH, s)
        to_y[slab(s), pl.ds(0, half_d)] = for_y[:, :half_d].astype(BF16)
        to_y[slab(s), pl.ds(half_d, width - half_d)] = (for_y[:, half_d:] + high_in[slab(s), :].astype(F32)).astype(BF16)
        send(S_Y, s, to_y.at[slab(s), :], from_y.at[slab(s), :], y_mate)

    def scatter_own(s):
        arrived(S_X, s)
        arrived(S_Y, s)
        total = both(s, 0) + from_x[slab(s), :].astype(F32) + from_y[slab(s), :].astype(F32)
        if s:
            to_z[slab(s), :] = total.astype(BF16)
            send(S_Z, s, to_z.at[slab(s), :], from_z.at[slab(s), :], z_mate(s))
        else:
            kept[...] = total

    for s in range(1, planes):
        send(Z_ROWS, s, block(0, 0, 0), block(s, 0, 0), z_mate(planes - s))
    stages = [(gather_own, 0), (gather_side, 1), (gather_diag, 2), (compute, 3), (scatter_diag, 4), (scatter_side, 5), (scatter_own, 6)]
    order = []
    for place, (stage, tick) in enumerate(stages):
        for s in range(planes):
            order.append((s + tick, place == 3, tick, s, stage))
    for _, _, _, s, stage in sorted(order, key=lambda item: item[:4]):
        stage(s)
    total = kept[...]
    for s in range(1, planes):
        arrived(S_Z, s)
        total = total + from_z[slab(s), :].astype(F32)
    out[...] = total.astype(BF16)
    for copy in copies.values():
        copy.wait_send()


def body(tokens, routes, gate_weights, w_gate, w_up, w_down):
    devices = lax.axis_size("ep")
    rows, width = tokens.shape
    hidden = w_gate.shape[2]
    planes = devices // (2 * PLANE)
    wide = width + pack_width(devices // 2)
    half_d = width // 256 * 128
    slab = pltpu.VMEM((planes * rows, width), BF16)
    anywhere, vmem = pl.BlockSpec(memory_space=pl.ANY), pl.BlockSpec(memory_space=pltpu.VMEM)
    return pl.pallas_call(
        functools.partial(kernel, devices),
        out_shape=jax.ShapeDtypeStruct((rows, width), BF16),
        in_specs=[anywhere, vmem, vmem, anywhere, anywhere, anywhere],
        out_specs=vmem,
        scratch_shapes=[
            pltpu.VMEM((devices * rows, wide), BF16),
            pltpu.VMEM((width, hidden), BF16),
            pltpu.VMEM((width, hidden), BF16),
            pltpu.VMEM((hidden, width), BF16),
            pltpu.VMEM((2 * PLANE * rows, hidden), BF16),
            pltpu.VMEM((devices // 2 * rows, width), F32),
            pltpu.VMEM((devices // 2 * rows, width), BF16),
            pltpu.VMEM((devices // 2 * rows, width), BF16),
            slab,
            pltpu.VMEM((planes * rows, half_d), BF16),
            pltpu.VMEM((planes * rows, width - half_d), BF16),
            slab, slab, slab, slab, slab, slab,
            pltpu.VMEM((rows, width), F32),
            pltpu.SemaphoreType.DMA((4,)),
            pltpu.SemaphoreType.DMA((KINDS, planes)),
            pltpu.SemaphoreType.DMA((KINDS, planes)),
        ],
        compiler_params=pltpu.CompilerParams(
            collective_id=0, has_side_effects=True, vmem_limit_bytes=60 * 1024 * 1024
        ),
    )(tokens, routes, gate_weights, w_gate, w_up, w_down)


def solution(mesh):
    placed = (
        P(("rep", "ep"), None),
        P(("rep", "ep"), None),
        P(("rep", "ep"), None),
        P("ep", None, None),
        P("ep", None, None),
        P("ep", None, None),
    )
    return jax.shard_map(
        body, mesh=mesh, in_specs=placed, out_specs=P(("rep", "ep"), None), check_vma=False
    )
```

time: 236 us -> 60.5 us (0.26)
  waiting for transfers between devices: 161 us -> 0 us
  Pallas kernels: 0 us -> 55.9 us
  blocking collectives: 44.3 us -> 0 us
  matrix products: 15.3 us -> 0 us
  between operations: 13.4 us -> 0.01 us
  local copies, waits for them, and re-layouts: 1.75 us -> 4.26 us
    reduce_scatter x1 -> x0, waiting for transfers between devices: 140 us -> none  [body(): lax.psum_scatter(partial_value.astype(jnp.bfloat16), 'ep', scatter_dimens...]
    pallas_call x0 -> x1, Pallas kernels: none -> 55.9 us  [body(): pl.pallas_call(functools.partial(kernel, devices), out_shape=jax.ShapeDty...]
    all_gather x1 -> x0, blocking collectives: 44.3 us -> none  [body(): all_gates = lax.all_gather(gates, 'ep', axis=0, tiled=True)]
    all_gather x1 -> x0, waiting for transfers between devices: 20 us -> none  [body(): rows = lax.all_gather(tokens, 'ep', axis=0, tiled=True)]
    dot_general x2 -> x0, matrix products: 15.3 us -> none  [the longest x1 10.1 us: body(): jnp.dot(hidden, w_down[0], preferred_element_type=jnp.float32)]
    unnamed x2 -> x3, local copies, waits for them, and re-layouts: 1.52 us -> 4.26 us
  transfers between devices with their start and end apart: 2 -> 0, of which waited for: 2 -> 0; matrix products, arithmetic and copies ran while one was open for 1% -> 0% of each run, Pallas kernels for 0% -> 0%
where the time goes in v2:
time: 60.5 us; the launch traced here: 60.2 us
  Pallas kernels  55.9 us (92%)
  local copies, waits for them, and re-layouts  4.26 us (7%)
    pallas_call x1, Pallas kernels, body(): pl.pallas_call(functools.partial(kernel, devices), out_shape=jax.ShapeDty...  55.9 us
    unnamed x3, local copies, waits for them, and re-layouts  4.26 us

profile of v2, /device:TPU:0, one launch (start us, length us, event | category | flops | bytes accessed | tf_op | source)
XLA Modules:
  0.0 60.2 jit_solution(17985649449722431908)
XLA Ops:
  0.0 1.4 %copy.7.routes = s32[16,8]{1,0:T(8,128)} copy(s32[16,8]{0,1:T(8,128)} %param.7) | data formatting | bytes 1024 | tf_op args[1]
  1.4 1.4 %copy.8.weights = f32[16,8]{1,0:T(8,128)} copy(f32[16,8]{0,1:T(8,128)} %param.8) | data formatting | bytes 1024 | tf_op args[2]
  2.7 55.9 %shard_map.64 = bf16[16,3584]{1,0:T(8,128)(2,1)} custom-call(bf16[16,3584]{1,0:T(8,128)(2,1)} %tokens.1, s32[16,8]{1,0:T(8,128)} %copy.7.routes, f32[16,8]{1,0:T(8,128)} %copy.8.weights, bf16[1,3584,512]{2,1,0:T(8,128)(2,1)} %w_gate.1, bf16[1,3584,512]{2,1,0:T(8,128)(2,1)} %w_up.1, bf16[1,512,3584]{2,1,0:T(8,128)(2,1)} %w_down.1), custom_call_target="tpu_custom_call" | custom-call | tf_op jit(solution)/shard_map/pallas_call | solution.py:211
  58.6 1.6 %copy.10 = bf16[16,3584]{1,0:T(8,128)(2,1)} copy(bf16[16,3584]{1,0:T(8,128)(2,1)} %shard_map.64) | data formatting | bytes 229376

commit v3 on v2

--- a/solution.py
+++ b/solution.py
@@ -52,7 +52,12 @@
     z, inside = me // (2 * PLANE), me % (2 * PLANE)
 
     def z_mate(step):
-        return ((z + step) % planes) * (2 * PLANE) + inside
+        other, bit = z, 1
+        while bit < planes:
+            if step & bit:
+                other = other + bit * (1 - 2 * ((z // bit) % 2))
+            bit *= 2
+        return other * (2 * PLANE) + inside
 
     loads = [
         pltpu.make_async_copy(tokens, tok.at[pl.ds(0, rows), pl.ds(0, width)], load_sem.at[0]),
@@ -66,7 +71,7 @@
     mates = [twin, x_mate, y_mate] + [z_mate(s) for s in range(1, planes)]
     for mate in mates:
         pl.semaphore_signal(barrier, inc=1, device_id={"ep": mate}, device_id_type=pl.DeviceIdType.MESH)
-    tok[pl.ds(0, rows), pl.ds(width, wide - width)] = packed_gates(routes[...], weights[...], expert_count, wide - width)
+    tok[pl.ds(0, rows), pl.ds(width, wide - width)] = packed_gates(routes[...].T, weights[...].T, expert_count, wide - width)
     loads[0].wait()
     pl.semaphore_wait(barrier, len(mates))
 
@@ -182,13 +187,13 @@
             kept[...] = total
 
     for s in range(1, planes):
-        send(Z_ROWS, s, block(0, 0, 0), block(s, 0, 0), z_mate(planes - s))
-    stages = [(gather_own, 0), (gather_side, 1), (gather_diag, 2), (compute, 3), (scatter_diag, 4), (scatter_side, 5), (scatter_own, 6)]
+        send(Z_ROWS, s, block(0, 0, 0), block(s, 0, 0), z_mate(s))
     order = []
-    for place, (stage, tick) in enumerate(stages):
-        for s in range(planes):
-            order.append((s + tick, place == 3, tick, s, stage))
-    for _, _, _, s, stage in sorted(order, key=lambda item: item[:4]):
+    for s in range(planes):
+        late = 5 + (s + planes - 1) % planes
+        order += [(s, 3, s, gather_own), (s + 1, 4, s, gather_side), (s + 2, 5, s, gather_diag), (s + 3, 6, s, compute)]
+        order += [(late, 2, s, scatter_diag), (late + 1, 1, s, scatter_side), (late + 2, 0, s, scatter_own)]
+    for _, _, s, stage in sorted(order, key=lambda item: item[:3]):
         stage(s)
     total = kept[...]
     for s in range(1, planes):
@@ -234,7 +239,7 @@
         compiler_params=pltpu.CompilerParams(
             collective_id=0, has_side_effects=True, vmem_limit_bytes=60 * 1024 * 1024
         ),
-    )(tokens, routes, gate_weights, w_gate, w_up, w_down)
+    )(tokens, routes.T, gate_weights.T, w_gate, w_up, w_down)
 
 
 def solution(mesh):

time: 60.5 us -> 57.7 us (0.954)
  local copies, waits for them, and re-layouts: 4.26 us -> 1.55 us
    unnamed x3 -> x1, local copies, waits for them, and re-layouts: 4.26 us -> 1.55 us
where the time goes in v3:
time: 57.7 us; the launch traced here: 57.5 us
  Pallas kernels  56 us (97%)
  local copies, waits for them, and re-layouts  1.55 us (3%)
    pallas_call x1, Pallas kernels, body(): pl.pallas_call(functools.partial(kernel, devices), out_shape=jax.ShapeDty...  56 us
    unnamed x1, local copies, waits for them, and re-layouts  1.55 us

profile of v3, /device:TPU:0, one launch (start us, length us, event | category | flops | bytes accessed | tf_op | source)
XLA Modules:
  0.0 57.5 jit_solution(10695749067812746148)
XLA Ops:
  0.0 56.0 %shard_map.64 = bf16[16,3584]{1,0:T(8,128)(2,1)} custom-call(bf16[16,3584]{1,0:T(8,128)(2,1)} %tokens.1, s32[8,16]{1,0:T(8,128)} %bitcast.2, f32[8,16]{1,0:T(8,128)} %bitcast.3, bf16[1,3584,512]{2,1,0:T(8,128)(2,1)} %w_gate.1, bf16[1,3584,512]{2,1,0:T(8,128)(2,1)} %w_up.1, bf16[1,512,3584]{2,1,0:T(8,128)(2,1)} %w_down.1), custom_call_target="tpu_custom_call" | custom-call | tf_op jit(solution)/shard_map/pallas_call | solution.py:216
  56.0 1.6 %copy.8 = bf16[16,3584]{1,0:T(8,128)(2,1)} copy(bf16[16,3584]{1,0:T(8,128)(2,1)} %shard_map.64) | data formatting | bytes 229376
